TPU v7x, 32 devices: a 4x4x1 block of a 4x4x8 slice. The times are simulated.
32 devices in a mesh: replica: 1 (over z), data2: 4 (over y), data: 8 (over x, core).
Axes of the slice: x: 4, y: 4, z: 1, core: 2. Of those that a mesh axis runs over, the one named last changes fastest.
The devices are a block of a 4x4x8 slice.
Arguments:
- q_hidden: bfloat16 [32, 32, 1024], P(('replica', 'data2', 'data'))
- d_hidden: bfloat16 [32, 8192, 1024], P(('replica', 'data2', 'data'))
- w_proj: bfloat16 [1024, 128], replicated
- q_mask: int32 [32, 32], P(('replica', 'data2', 'data'))
- d_mask: int32 [32, 8192], P(('replica', 'data2', 'data'))
- temperature: float32 [], replicated
Outputs:
- output 1: float32 [32], P(('replica', 'data2', 'data'))
- output 2: float32 [1], P('replica')
All inputs are finite; a program needn't handle non-finite values.
Results may differ from a plain program's by a relative error of at most 0.00151.
Values are sent between devices in bfloat16 or wider.
A program may use at most 768 MiB of HBM per device.

v0:
```python
import jax
import jax.numpy as jnp
from jax import lax
from jax.sharding import PartitionSpec as P

NORM_EPS = 1e-6
GROUP_AXES = ('data2', 'data')
ROW_AXES = ('replica', 'data2', 'data')


def project(hidden, w_proj):
    proj_f32 = jnp.einsum('bld,de->ble', hidden, w_proj, preferred_element_type=jnp.float32)
    row_norm = jnp.sqrt(jnp.sum(proj_f32 * proj_f32, axis=-1, keepdims=True) + NORM_EPS)
    return (proj_f32 / row_norm).astype(jnp.bfloat16)


def block_scores(q_block, d_tok, d_valid):
    sim_vals = jnp.einsum('qtd,psd->qtps', q_block, d_tok, preferred_element_type=jnp.float32)
    sim_vals = jnp.where(d_valid[None, None], sim_vals, -jnp.inf)
    return jnp.sum(jnp.max(sim_vals, axis=-1), axis=1)


def row_losses(row_scores, value_a11, my_index, per_dev):
    logits = row_scores / value_a11
    row_max = jnp.max(logits, axis=1, keepdims=True)
    log_norm = row_max[:, 0] + jnp.log(jnp.sum(jnp.exp(logits - row_max), axis=1))
    pos_tile = lax.dynamic_slice_in_dim(logits, my_index * per_dev, per_dev, axis=1)
    return log_norm - jnp.diagonal(pos_tile)


def solution(mesh):
    outer_size = mesh.shape['data2']
    inner_size = mesh.shape['data']
    group_size = outer_size * inner_size

    def device_fn(q_hidden, d_hidden, w_proj, q_mask, d_mask, value_a11):
        per_dev, q_len = q_mask.shape
        proj_dim = w_proj.shape[1]
        q_tok = jnp.where(q_mask[:, :, None] > 0, project(q_hidden, w_proj), jnp.zeros((), jnp.bfloat16))
        d_tok = project(d_hidden, w_proj)
        d_valid = d_mask > 0
        all_q = lax.all_gather(q_tok, GROUP_AXES, axis=0, tiled=True)
        all_q = all_q.reshape(group_size, per_dev, q_len, proj_dim)

        def score_block(q_block):
            return block_scores(q_block, d_tok, d_valid)

        col_scores = lax.map(score_block, all_q).reshape(outer_size, inner_size, per_dev, per_dev)
        col_scores = lax.all_to_all(col_scores, 'data', 1, 1, tiled=True)
        col_scores = lax.all_to_all(col_scores, 'data2', 0, 0, tiled=True)
        row_scores = jnp.transpose(col_scores, (2, 0, 1, 3)).reshape(per_dev, group_size * per_dev)
        my_index = lax.axis_index('data2') * inner_size + lax.axis_index('data')
        loss_rows = row_losses(row_scores, value_a11, my_index, per_dev)
        loss_mean = lax.psum(jnp.sum(loss_rows), GROUP_AXES) / (group_size * per_dev)
        return loss_rows, loss_mean.reshape(1)

    return jax.shard_map(
        device_fn,
        mesh=mesh,
        in_specs=(P(ROW_AXES), P(ROW_AXES), P(), P(ROW_AXES), P(ROW_AXES), P()),
        out_specs=(P(ROW_AXES), P('replica')),
        check_vma=False,
    )
```

profile of v0, /device:TPU:97, one launch (start us, length us, event | category | flops | bytes accessed | tf_op | source)
XLA Modules:
  0.0 208.0 jit_solution(7301683981030546396)
XLA Ops:
  0.7 0.9 copy-done
  1.6 13.3 %multiply_reduce_fusion = (f32[8192]{0:T(1024)S(1)}, f32[8192,128]{0,1:T(8,128)}) fusion(bf16[1024,128]{1,0:T(8,128)(2,1)S(1)} %copy-done, bf16[1,8192,1024]{2,1,0:T(8,128)(2,1)} %param.9), kind=kOutput, calls=%fused_computation.9 | convolution fusion | flops 2149572608 | bytes 21266432 | tf_op jit(solution)/shard_map/bld,de->ble/dot_general | solution.py:12
  14.9 3.9 %fusion.9 = bf16[1,8192,128]{1,2,0:T(8,128)(2,1)} fusion(f32[8192,128]{0,1:T(8,128)} %get-tuple-element.57, f32[8192]{0:T(1024)S(1)} %add_sqrt_fusion), kind=kLoop, calls=%fused_computation.10 | loop fusion | flops 2097152 | bytes 6324224 | tf_op jit(solution)/shard_map/convert_element_type | solution.py:14
  18.8 3.2 %copy.11 = bf16[1,8192,128]{2,1,0:T(8,128)(2,1)S(1)} copy(bf16[1,8192,128]{1,2,0:T(8,128)(2,1)} %fusion.9) | data formatting | bytes 4194304 | tf_op jit(solution)/shard_map/while | solution.py:48
  22.4 32.5 %all-gather = bf16[1024,128]{1,0:T(8,128)(2,1)S(1)} all-gather(bf16[32,128]{1,0:T(8,128)(2,1)S(1)} %fusion.12), channel_id=2, replica_groups=mesh['replica'=1,'data2'=4,'data'=8] {'data2','data'}, dimensions={0}, use_global_device_ids=true | all-gather | bytes 270336 | tf_op jit(solution)/shard_map/all_gather | solution.py:42
  55.0 76.3 %while.10 = (s32[]{:T(128)}, f32[32,1,1]{0,2,1:T(1,128)S(1)}, pred[1,8192]{1,0:T(4,128)(4,1)S(1)}, bf16[32,1,32,128]{3,2,1,0:T(8,128)(2,1)S(1)}, bf16[1,8192,128...) while((s32[]{:T(128)}, f32[32,1,1]{0,2,1:T(1,128)S(1)}, ...), condition=%wide.region_5.6_spmd, body=%wide.region_2.5_spmd.sunk | while | flops 67633152 | bytes 2130294 | solution.py:48
  55.1 0.9 fusion.22
  57.5 0.9 fusion.22
  59.0 0.8 dynamic_update_slice.5
  59.8 0.9 fusion.22
  61.4 0.8 dynamic_update_slice.5
  62.2 0.9 fusion.22
  63.8 0.8 dynamic_update_slice.5
  64.6 0.9 fusion.22
  66.1 0.8 dynamic_update_slice.5
  67.0 0.9 fusion.22
  68.5 0.8 dynamic_update_slice.5
  69.4 0.9 fusion.22
  71.8 0.9 fusion.22
  74.1 0.9 fusion.22
  75.7 0.8 dynamic_update_slice.5
  76.5 0.9 fusion.22
  78.1 0.8 dynamic_update_slice.5
  78.9 0.9 fusion.22
  80.5 0.8 dynamic_update_slice.5
  81.3 0.9 fusion.22
  82.8 0.8 dynamic_update_slice.5
  83.7 0.9 fusion.22
  85.2 0.8 dynamic_update_slice.5
  86.1 0.9 fusion.22
  87.6 0.8 dynamic_update_slice.5
  88.5 0.9 fusion.22
  90.0 0.8 dynamic_update_slice.5
  90.8 0.9 fusion.22
  93.2 0.9 fusion.22
  95.6 0.9 fusion.22
  98.0 0.9 fusion.22
  99.5 0.8 dynamic_update_slice.5
  100.4 0.9 fusion.22
  101.9 0.8 dynamic_update_slice.5
  102.8 0.9 fusion.22
  105.1 0.9 fusion.22
  106.7 0.8 dynamic_update_slice.5
  107.5 0.9 fusion.22
  109.1 0.8 dynamic_update_slice.5
  109.9 0.9 fusion.22
  111.5 0.8 dynamic_update_slice.5
  112.3 0.9 fusion.22
  114.7 0.9 fusion.22
  117.1 0.9 fusion.22
  118.6 0.8 dynamic_update_slice.5
  119.5 0.9 fusion.22
  121.8 0.9 fusion.22
  124.2 0.9 fusion.22
  126.6 0.9 fusion.22
  128.1 0.8 dynamic_update_slice.5
  129.0 0.9 fusion.22
  130.5 0.8 dynamic_update_slice.5
  133.2 9.8 %all-to-all-start = ((f32[4,8,1,1]{0,3,2,1:T(1,128)}), f32[4,8,1,1]{0,3,2,1:T(1,128)S(1)}, u32[]{:S(2)}, u32[]{:S(2)}) async-start(f32[4,8,1,1]{0,3,2,1:T(1,128)} %copy.12), calls=%async_computation | async-start | bytes 8192 | tf_op jit(solution)/shard_map/all_to_all | solution.py:49
  143.7 3.8 %all-to-all-done = f32[4,8,1,1]{0,3,2,1:T(1,128)S(1)} async-done(((f32[4,8,1,1]{0,3,2,1:T(1,128)}), f32[4,8,1,1]{0,3,2,1:T(1,128)S(1)}, u32[]{:S(2)}, u32[]{:S(2)}) %all-to-all-start) | async-done | bytes 160 | tf_op jit(solution)/shard_map/all_to_all | solution.py:49
  148.2 3.3 %all-to-all-start.1 = ((f32[4,8,1,1]{1,3,2,0:T(1,128)}), f32[4,8,1,1]{1,3,2,0:T(1,128)S(1)}, u32[]{:S(2)}, u32[]{:S(2)}) async-start(f32[4,8,1,1]{1,3,2,0:T(1,128)} %copy.13), calls=%async_computation.1 | async-start | bytes 4096 | tf_op jit(solution)/shard_map/all_to_all | solution.py:50
  151.5 3.8 %all-to-all-done.1 = f32[4,8,1,1]{1,3,2,0:T(1,128)S(1)} async-done(((f32[4,8,1,1]{1,3,2,0:T(1,128)}), f32[4,8,1,1]{1,3,2,0:T(1,128)S(1)}, u32[]{:S(2)}, u32[]{:S(2)}) %all-to-all-start.1) | async-done | bytes 160 | tf_op jit(solution)/shard_map/all_to_all | solution.py:50
  156.0 1.9 fusion.13
  160.5 44.5 %psum.7 = f32[]{:T(128)} all-reduce(f32[]{:T(128)} %bitcast.11), channel_id=1, replica_groups=mesh['replica'=1,'data2'=4,'data'=8] {'data2','data'}, use_global_device_ids=true, to_apply=%region_8.9 | all-reduce | flops 1 | bytes 8 | tf_op jit(solution)/shard_map/psum | solution.py:54
  (98 shorter events, 35.8 us)
Async XLA Ops:
  0.6 1.0 copy-start
  14.9 7.1 %copy-start.1 = (bf16[1,32,1024]{2,1,0:T(8,128)(2,1)S(1)}, bf16[1,32,1024]{2,1,0:T(8,128)(2,1)}, u32[]{:S(2)}) copy-start(bf16[1,32,1024]{2,1,0:T(8,128)(2,1)} %param.8) | copy-start | bytes 196612
  14.9 7.4 %copy-start.3 = (s32[1,32]{1,0:T(1,128)S(1)}, s32[1,32]{1,0:T(1,128)}, u32[]{:S(2)}) copy-start(s32[1,32]{1,0:T(1,128)} %param.11) | copy-start | bytes 388
  14.9 40.1 %copy-start.2 = (s32[1,8192]{1,0:T(1,128)S(1)}, s32[1,8192]{1,0:T(1,128)}, u32[]{:S(2)}) copy-start(s32[1,8192]{1,0:T(1,128)} %param.12) | copy-start | bytes 98308
  133.2 14.3 %all-to-all-start = ((f32[4,8,1,1]{0,3,2,1:T(1,128)}), f32[4,8,1,1]{0,3,2,1:T(1,128)S(1)}, u32[]{:S(2)}, u32[]{:S(2)}) async-start(f32[4,8,1,1]{0,3,2,1:T(1,128)} %copy.12), calls=%async_computation | async-start | bytes 8192 | tf_op jit(solution)/shard_map/all_to_all | solution.py:49
  148.2 7.2 %all-to-all-start.1 = ((f32[4,8,1,1]{1,3,2,0:T(1,128)}), f32[4,8,1,1]{1,3,2,0:T(1,128)S(1)}, u32[]{:S(2)}, u32[]{:S(2)}) async-start(f32[4,8,1,1]{1,3,2,0:T(1,128)} %copy.13), calls=%async_computation.1 | async-start | bytes 4096 | tf_op jit(solution)/shard_map/all_to_all | solution.py:50
where the time goes:
time: 209 us; the launch traced here: 208 us
  blocking collectives  77.1 us (37%)
  matrix products  43.1 us (21%)
  local copies, waits for them, and re-layouts  30.8 us (15%)
  other arithmetic  29.7 us (14%)
  starting transfers between devices  13.1 us (6%)
  waiting for transfers between devices  7.67 us (4%)
  between operations  6.31 us (3%)
    psum x1, blocking collectives, device_fn(): lax.psum(jnp.sum(loss_rows), GROUP_AXES) / (group_size * per_dev)  44.5 us
    all_gather x1, blocking collectives, device_fn(): all_q = lax.all_gather(q_tok, GROUP_AXES, axis=0, tiled=True)  32.5 us
    dot_general x32, matrix products, block_scores(): jnp.einsum('qtd,psd->qtps', q_block, d_tok, preferred_element_type=jnp.fl...  29.6 us
    dynamic_update_slice x32, local copies, waits for them, and re-layouts, device_fn(): lax.map(score_block, all_q)  24 us
    reduce_sum x32, other arithmetic, block_scores(): return jnp.sum(jnp.max(sim_vals, axis=-1), axis=1)  19.6 us
    dot_general x2, matrix products, project(): jnp.einsum('bld,de->ble', hidden, w_proj, preferred_element_type=jnp.floa...  13.5 us
    all_to_all x1, starting transfers between devices, device_fn(): col_scores = lax.all_to_all(col_scores, 'data', 1, 1, tiled=True)  9.8 us
  transfers between devices with their start and end apart: 2, of which 2 were waited for; matrix products, arithmetic and copies ran while one was open for 0% of the time, Pallas kernels for 0%

commit v1 on v0

v1 whole, which is shorter than its diff:
```python
import functools

import jax
import jax.numpy as jnp
from jax import lax
from jax.experimental import pallas as pl
from jax.experimental.pallas import tpu as pltpu
from jax.sharding import PartitionSpec as P

NORM_EPS = 1e-6
ROW_AXES = ('replica', 'data2', 'data')
MASKED = -1e30
CORES = 2
CHUNK = 512
DEPTH = 6
UNROLL = 2
SEND_STEP = 3
SCORE_ROWS = 4096
GROUP = 8
MESH = pl.DeviceIdType.MESH


def ring_distance(step, size):
    return min(step, size - step)


def peer_offsets(outer, inner):
    chips = inner // CORES
    offsets = [(a, b, c) for a in range(outer) for b in range(chips) for c in range(CORES)]
    return sorted(offsets, key=lambda o: (ring_distance(o[0], outer) + ring_distance(o[1], chips), o[2], o[0], o[1]))


def kernel(outer, inner, q_hbm, d_ref, w_hbm, qm_hbm, dm_hbm, out_ref,
           hidden, raw, tokens, all_q, acc, column, table, senders, q_ref, w_ref, qm_ref, dm_ref,
           small_sem, chunk_sem, send_sem, q_sem, s_send_sem, s_sem):
    group_size = outer * inner
    chips = inner // CORES
    q_len, proj = all_q.shape[1], w_ref.shape[1]
    n_chunks = hidden.shape[0]
    offsets = peer_offsets(outer, inner)
    my_outer, my_inner = lax.axis_index('data2'), lax.axis_index('data')
    my_chip, my_core = my_inner // CORES, my_inner % CORES
    me = my_outer * inner + my_inner

    def device(offset, sign):
        a, b, c = offset
        a = lax.rem(my_outer + sign * a + outer, outer)
        b = lax.rem(my_chip + sign * b + chips, chips)
        c = lax.rem(my_core + sign * c + CORES, CORES)
        return a, b * CORES + c

    def device_id(offset):
        a, b = device(offset, 1)
        return {'data2': a, 'data': b}

    def row_of(p):
        per_row = 128 // q_len
        row = p % per_row * (group_size // per_row) + p // per_row
        return slice(row, row + 1)

    smalls = [pltpu.make_async_copy(src, dst, small_sem.at[i]) for i, (src, dst) in enumerate(
        [(q_hbm, q_ref), (w_hbm, w_ref), (qm_hbm, qm_ref), (dm_hbm, dm_ref)])]
    for copy in smalls:
        copy.start()

    def fetch(b):
        return pltpu.make_async_copy(d_ref.at[0, pl.ds(b * CHUNK, CHUNK), :], hidden.at[b], chunk_sem.at[b])

    barrier = pltpu.get_barrier_semaphore()
    for offset in offsets[1:]:
        pl.semaphore_signal(barrier, inc=1, device_id=device_id(offset), device_id_type=MESH)

    for b in range(DEPTH):
        fetch(b).start()

    for p in range(group_size):
        a, b = device(offsets[p], -1)
        senders[row_of(p), :] = jnp.full((1, 128), a * inner + b, jnp.int32)
    for copy in smalls:
        copy.wait()

    y = jnp.dot(q_ref[0], w_ref[...], preferred_element_type=jnp.float32)
    unit = y * lax.rsqrt(jnp.sum(y * y, axis=-1, keepdims=True) + NORM_EPS)
    row = lax.broadcasted_iota(jnp.int32, (q_len, q_len), 0)
    col = lax.broadcasted_iota(jnp.int32, (q_len, q_len), 1)
    weight = jnp.sum(jnp.where(row == col, qm_ref[...], 0).astype(jnp.float32), axis=1, keepdims=True)
    all_q[0] = jnp.where(weight > 0, unit, 0.0).astype(jnp.bfloat16)

    def q_copy(p):
        return pltpu.make_async_remote_copy(
            src_ref=all_q.at[0], dst_ref=all_q.at[p], send_sem=send_sem, recv_sem=q_sem.at[p // GROUP],
            device_id=device_id(offsets[p]), device_id_type=MESH)

    def project(b, slot):
        raw[slot] = jnp.dot(hidden[b], w_ref[...], preferred_element_type=jnp.float32)

    def normalise(b, slot):
        y = raw[slot]
        scale = lax.rsqrt(jnp.sum(y * y, axis=-1, keepdims=True) + NORM_EPS)
        rows = pl.ds(pl.multiple_of(b * CHUNK, CHUNK), CHUNK)
        tokens[rows, :proj] = (y * scale).astype(jnp.bfloat16)
        mask = dm_ref[:, rows]
        bias = jnp.where(mask > 0, 0.0, MASKED)
        for c in range(0, CHUNK, 128):
            block = jnp.broadcast_to(bias[:, c:c + 128], (128, 128)).T
            tokens[pl.ds(pl.multiple_of(b * CHUNK + c, 128), 128), proj:] = block.astype(jnp.bfloat16)

    def step(i, first):
        for u in range(UNROLL):
            fetch(i * UNROLL + u).wait()
        for u in range(UNROLL):
            @pl.when(i * UNROLL + u + DEPTH < n_chunks)
            def _():
                fetch(i * UNROLL + u + DEPTH).start()
        if not first:
            for u in range(UNROLL):
                normalise((i - 1) * UNROLL + u, lax.rem(i + 1, 2) * UNROLL + u)
        for u in range(UNROLL):
            project(i * UNROLL + u, lax.rem(i, 2) * UNROLL + u)

    steps = n_chunks // UNROLL
    step(0, True)

    @pl.loop(1, SEND_STEP)
    def _(i):
        step(i, False)

    pl.semaphore_wait(barrier, group_size - 1)
    for p in range(1, group_size):
        q_copy(p).start()

    @pl.loop(SEND_STEP, steps)
    def _(i):
        step(i, False)

    for u in range(UNROLL):
        normalise((steps - 1) * UNROLL + u, (steps - 1) % 2 * UNROLL + u)

    lane = lax.broadcasted_iota(jnp.int32, (GROUP * q_len, proj), 1)
    ones = jnp.where(lane == 0, 1.0, 0.0).astype(jnp.bfloat16)

    @pl.loop(0, group_size // GROUP)
    def _(g):
        def arrived(count):
            view = all_q.at[pl.ds(0, count)]
            pltpu.make_async_copy(view, view, q_sem.at[g]).wait()

        @pl.when(g == 0)
        def _():
            arrived(GROUP - 1)

        @pl.when(g > 0)
        def _():
            arrived(GROUP)

        block = all_q[pl.ds(g * GROUP, GROUP)].reshape(GROUP * q_len, proj)
        block = jnp.concatenate([block, ones], axis=1)
        best = None
        for b in range(0, tokens.shape[0], SCORE_ROWS):
            sim = lax.dot_general(tokens[b:b + SCORE_ROWS, :], block, (((1,), (1,)), ((), ())),
                                  preferred_element_type=jnp.float32)
            part = jnp.max(sim.reshape(SCORE_ROWS // 8, 8, GROUP * q_len), axis=0)
            best = part if best is None else jnp.maximum(best, part)
        acc[g] = best

    top = jnp.max(acc[...], axis=1).reshape(group_size * q_len // 128, 128)
    per_row = 128 // q_len
    n_rows = group_size // per_row
    lane = lax.broadcasted_iota(jnp.int32, (n_rows, 128), 1)
    mine = jnp.zeros((1, 128), jnp.float32)
    for k in range(per_row):
        total = jnp.sum(jnp.where(lane // q_len == k, top, 0.0), axis=1, keepdims=True)
        mine += jnp.sum(jnp.where(lane == senders[k * n_rows:(k + 1) * n_rows, :], total, 0.0), axis=0, keepdims=True)
    column[...] = mine

    def s_copy(p):
        return pltpu.make_async_remote_copy(
            src_ref=column, dst_ref=table.at[row_of(p), :], send_sem=s_send_sem, recv_sem=s_sem,
            device_id=device_id(offsets[p]), device_id_type=MESH)

    for p in range(group_size - 1, 0, -1):
        s_copy(p).start()

    sent = all_q.at[pl.ds(0, group_size - 1)]
    pltpu.make_async_copy(sent, sent, send_sem).wait()
    others = table.at[pl.ds(0, group_size - 1), :]
    pltpu.make_async_copy(others, others, s_sem).wait()
    pltpu.make_async_copy(others, others, s_send_sem).wait()

    rows = lax.broadcasted_iota(jnp.int32, (group_size, 128), 0)
    out_ref[0] = jnp.where(rows == 0, mine, table[...])
    out_ref[1] = senders[...].astype(jnp.float32)


def finish(outer, inner, scores_ref, temp_ref, rows_ref, mean_ref):
    group_size = outer * inner
    me = lax.axis_index('data2') * inner + lax.axis_index('data')
    logits = scores_ref[0] / temp_ref[0]
    peak = jnp.max(logits, axis=0, keepdims=True)
    log_norm = peak + jnp.log(jnp.sum(jnp.exp(logits - peak), axis=0, keepdims=True))
    lane = lax.broadcasted_iota(jnp.int32, (group_size, 128), 1)
    own = lane == scores_ref[1].astype(jnp.int32)
    loss = log_norm - jnp.sum(jnp.where(own, logits, 0.0), axis=0, keepdims=True)
    lane = lane[:1]
    rows_ref[0] = jnp.sum(jnp.where(lane == me, loss, 0.0))
    mean_ref[0] = jnp.sum(jnp.where(lane < group_size, loss, 0.0)) / group_size


def solution(mesh):
    outer, inner = mesh.shape['data2'], mesh.shape['data']
    group_size = outer * inner

    def device_fn(q_hidden, d_hidden, w_proj, q_mask, d_mask, temperature):
        q_len, width = q_hidden.shape[1:]
        d_len, proj = d_hidden.shape[1], w_proj.shape[1]
        n_chunks = d_len // CHUNK
        smem = pl.BlockSpec(memory_space=pltpu.SMEM)
        vmem = pl.BlockSpec(memory_space=pltpu.VMEM)
        scores = pl.pallas_call(
            functools.partial(kernel, outer, inner),
            out_shape=jax.ShapeDtypeStruct((2, group_size, 128), jnp.float32),
            in_specs=[pl.BlockSpec(memory_space=pl.ANY)] * 5,
            out_specs=vmem,
            scratch_shapes=[
                pltpu.VMEM((n_chunks, CHUNK, width), jnp.bfloat16),
                pltpu.VMEM((2 * UNROLL, CHUNK, proj), jnp.float32),
                pltpu.VMEM((d_len, 2 * proj), jnp.bfloat16),
                pltpu.VMEM((group_size, q_len, proj), jnp.bfloat16),
                pltpu.VMEM((group_size // GROUP, 8, GROUP * q_len), jnp.float32),
                pltpu.VMEM((1, 128), jnp.float32),
                pltpu.VMEM((group_size, 128), jnp.float32),
                pltpu.VMEM((group_size, 128), jnp.int32),
                pltpu.VMEM(q_hidden.shape, q_hidden.dtype),
                pltpu.VMEM(w_proj.shape, w_proj.dtype),
                pltpu.VMEM(q_mask.shape, q_mask.dtype),
                pltpu.VMEM(d_mask.shape, d_mask.dtype),
                pltpu.SemaphoreType.DMA((4,)),
                pltpu.SemaphoreType.DMA((n_chunks,)),
                pltpu.SemaphoreType.DMA,
                pltpu.SemaphoreType.DMA((group_size // GROUP,)),
                pltpu.SemaphoreType.DMA,
                pltpu.SemaphoreType.DMA,
            ],
            compiler_params=pltpu.CompilerParams(collective_id=0, has_side_effects=True,
                                                 vmem_limit_bytes=60 * 1024 * 1024),
            name='colbert_loss',
        )(q_hidden, d_hidden, w_proj, q_mask, d_mask)
        return pl.pallas_call(
            functools.partial(finish, outer, inner),
            out_shape=(jax.ShapeDtypeStruct((1,), jnp.float32),) * 2,
            in_specs=[vmem, smem],
            out_specs=(smem, smem),
            name='loss',
        )(scores, temperature.reshape(1))

    return jax.shard_map(
        device_fn,
        mesh=mesh,
        in_specs=(P(ROW_AXES), P(ROW_AXES), P(), P(ROW_AXES), P(ROW_AXES), P()),
        out_specs=(P(ROW_AXES), P('replica')),
        check_vma=False,
    )
```

time: 209 us -> 28.1 us (0.13)
  blocking collectives: 77.1 us -> 0 us
  matrix products: 43.1 us -> 0 us
  local copies, waits for them, and re-layouts: 30.8 us -> 0 us
  other arithmetic: 29.7 us -> 0 us
  Pallas kernels: 0 us -> 26.7 us
  starting transfers between devices: 13.1 us -> 0 us
  waiting for transfers between devices: 7.67 us -> 0 us
  between operations: 6.31 us -> 1.29 us
    psum x1 -> x0, blocking collectives: 44.5 us -> none  [device_fn(): lax.psum(jnp.sum(loss_rows), GROUP_AXES) / (group_size * per_dev)]
    dot_general x34 -> x0, matrix products: 43.1 us -> none  [the longest x32 29.6 us: block_scores(): jnp.einsum('qtd,psd->qtps', q_block, d_tok, preferred_element_type=jnp.fl...]
    all_gather x1 -> x0, blocking collectives: 32.5 us -> none  [device_fn(): all_q = lax.all_gather(q_tok, GROUP_AXES, axis=0, tiled=True)]
    pallas_call x0 -> x2, Pallas kernels: none -> 26.7 us  [the longest x1 25.2 us: device_fn(): pl.pallas_call(functools.partial(kernel, outer, inner), out_shape=jax.Sha...]
    dynamic_update_slice x32 -> x0, local copies, waits for them, and re-layouts: 24 us -> none  [device_fn(): lax.map(score_block, all_q)]
    reduce_sum x32 -> x0, other arithmetic: 19.6 us -> none  [block_scores(): return jnp.sum(jnp.max(sim_vals, axis=-1), axis=1)]
    all_to_all x2 -> x0, starting transfers between devices: 13.1 us -> none  [the longest x1 9.8 us: device_fn(): col_scores = lax.all_to_all(col_scores, 'data', 1, 1, tiled=True)]
    all_to_all x2 -> x0, waiting for transfers between devices: 7.67 us -> none  [the longest x1 3.85 us: device_fn(): col_scores = lax.all_to_all(col_scores, 'data2', 0, 0, tiled=True)]
  transfers between devices with their start and end apart: 2 -> 0, of which waited for: 2 -> 0; matrix products, arithmetic and copies ran while one was open for 0% -> 0% of each run, Pallas kernels for 0% -> 0%
where the time goes in v1:
time: 28.1 us; the launch traced here: 28 us
  Pallas kernels  26.7 us (95%)
  between operations  1.29 us (5%)
    pallas_call x1, Pallas kernels, device_fn(): pl.pallas_call(functools.partial(kernel, outer, inner), out_shape=jax.Sha...  25.2 us
    pallas_call x1, Pallas kernels, device_fn(): pl.pallas_call(functools.partial(finish, outer, inner), out_shape=(jax.Sh...  1.44 us

profile of v1, /device:TPU:97, one launch (start us, length us, event | category | flops | bytes accessed | tf_op | source)
XLA Modules:
  0.0 28.0 jit_solution(8841615760563323696)
XLA Ops:
  1.3 25.2 %colbert_loss.1.scores_ref = f32[2,32,128]{2,1,0:T(8,128)} custom-call(bf16[1,32,1024]{2,1,0:T(8,128)(2,1)} %q_hbm.1, bf16[1,8192,1024]{2,1,0:T(8,128)(2,1)} %d_ref.1, bf16[1024,128]{1,0:T(8,128)(2,1)} %w_hbm.1, s32[1,32]{1,0:T(1,128)} %qm_hbm.1, s32[1,8192]{1,0:T(1,128)} %dm_hbm.1), custom_call_target="tpu_custom_call" | custom-call | tf_op jit(solution)/shard_map/colbert_loss/pallas_call | solution.py:219
  26.5 1.4 %loss.1 = (f32[1]{0:T(128)}, f32[1]{0:T(128)}) custom-call(f32[2,32,128]{2,1,0:T(8,128)} %colbert_loss.1.scores_ref, f32[1]{0:T(128)} %bitcast.1.temp_ref), custom_call_target="tpu_custom_call" | custom-call | tf_op jit(solution)/shard_map/loss/pallas_call | solution.py:248

commit v2 on v1

v2 whole, which is shorter than its diff:
```python
import functools

import jax
import jax.numpy as jnp
from jax import lax
from jax.experimental import pallas as pl
from jax.experimental.pallas import tpu as pltpu
from jax.sharding import PartitionSpec as P

NORM_EPS = 1e-6
ROW_AXES = ('replica', 'data2', 'data')
MASKED = -1e30
CORES = 2
CHUNK = 512
DEPTH = 16
LEVELS = 2
RINGS = 1
FIRST = 2
STEPS = (1, 3, 4, 4, 4)
SEND_STEP = 2
SMALL_WAITS = ((0,), (1, 2, 3))
SCORE_ROWS = 4096
MESH = pl.DeviceIdType.MESH


def kernel(outer, inner, q_hbm, d_ref, w_hbm, qm_hbm, dm_hbm, out_ref,
           hidden, raw, tokens, all_q, acc, column, table, senders, q_ref, w_ref, qm_ref, dm_ref,
           small_sem, chunk_sem, send_sem, q_sem, s_send_sem, s_sem):
    part = all_q.shape[0] // (CORES * RINGS)
    group_size = outer * inner
    chips = inner // CORES
    q_len, proj = all_q.shape[1], w_ref.shape[1]
    n_chunks = hidden.shape[0]
    my_outer, my_inner = lax.axis_index('data2'), lax.axis_index('data')
    my_core = my_inner % CORES
    me = my_outer * inner + my_inner
    n_chips = group_size // CORES
    my_place = me // CORES
    my_ring = my_place // part
    my_slot = my_ring * CORES * part + my_place % part

    def chip_id(place):
        return {'data2': place // chips, 'data': place % chips * CORES + my_core}

    def other_chip(t):
        return t + 1 - (my_place + n_chips - 1 - t) // n_chips

    partner = {'data2': my_outer, 'data': my_inner + 1 - 2 * my_core}

    def row_of(p):
        per_row = 128 // q_len
        row = p % per_row * (group_size // per_row) + p // per_row
        return slice(row, row + 1)

    smalls = [pltpu.make_async_copy(src, dst, small_sem.at[i]) for i, (src, dst) in enumerate(
        [(w_hbm, w_ref), (q_hbm, q_ref), (qm_hbm, qm_ref), (dm_hbm, dm_ref)])]
    def fetch(b):
        return pltpu.make_async_copy(d_ref.at[0, pl.ds(b * CHUNK, CHUNK), :], hidden.at[b], chunk_sem.at[b])

    smalls[0].start()
    for b in range(FIRST):
        fetch(b).start(priority=min(b // FIRST, LEVELS - 1))
    barrier = pltpu.get_barrier_semaphore()
    for target in [chip_id(other_chip(t)) for t in range(n_chips - 1)] + [partner]:
        pl.semaphore_signal(barrier, inc=1, device_id=target, device_id_type=MESH)
    for copy in smalls[1:]:
        copy.start()
    for b in range(FIRST, DEPTH):
        fetch(b).start(priority=min(b // FIRST, LEVELS - 1))

    for p in range(group_size):
        place = p // (CORES * part) * part + p % part
        core = my_core if p // part % CORES == 0 else 1 - my_core
        senders[row_of(p), :] = jnp.full((1, 128), place * CORES + core, jnp.int32)
    def query():
        y = jnp.dot(q_ref[0], w_ref[...], preferred_element_type=jnp.float32)
        unit = y * lax.rsqrt(jnp.sum(y * y, axis=-1, keepdims=True) + NORM_EPS)
        row = lax.broadcasted_iota(jnp.int32, (q_len, q_len), 0)
        col = lax.broadcasted_iota(jnp.int32, (q_len, q_len), 1)
        weight = jnp.sum(jnp.where(row == col, qm_ref[...], 0).astype(jnp.float32), axis=1, keepdims=True)
        all_q[my_slot] = jnp.where(weight > 0, unit, 0.0).astype(jnp.bfloat16)

    def q_copy(t):
        return pltpu.make_async_remote_copy(
            src_ref=all_q.at[my_slot], dst_ref=all_q.at[my_slot], send_sem=send_sem.at[0], recv_sem=q_sem.at[my_ring * CORES],
            device_id=chip_id(other_chip(t)), device_id_type=MESH)

    def forward(r):
        return pltpu.make_async_remote_copy(
            src_ref=all_q.at[pl.ds(CORES * r * part, part)], dst_ref=all_q.at[pl.ds((CORES * r + 1) * part, part)],
            send_sem=send_sem.at[1 + r], recv_sem=q_sem.at[CORES * r + 1], device_id=partner, device_id_type=MESH)

    def project(b):
        raw[b] = jnp.dot(hidden[b], w_ref[...], preferred_element_type=jnp.float32)

    def normalise(b):
        y = raw[b]
        scale = lax.rsqrt(jnp.sum(y * y, axis=-1, keepdims=True) + NORM_EPS)
        rows = slice(b * CHUNK, (b + 1) * CHUNK)
        tokens[rows, :proj] = (y * scale).astype(jnp.bfloat16)
        bias = jnp.where(dm_ref[:, rows] > 0, 0.0, MASKED)
        for c in range(0, CHUNK, 128):
            block = jnp.broadcast_to(bias[:, c:c + 128], (128, 128)).T
            tokens[b * CHUNK + c:b * CHUNK + c + 128, proj:] = block.astype(jnp.bfloat16)

    chunks, ready = list(range(n_chunks)), []
    for i, count in enumerate(STEPS):
        now, chunks = chunks[:count], chunks[count:]
        if i == SEND_STEP:
            pl.semaphore_wait(barrier, n_chips)
            for t in reversed(range(n_chips - 1)):
                q_copy(t).start()
        for b in now:
            fetch(b).wait()
            if b + DEPTH < n_chunks:
                fetch(b + DEPTH).start()
        if i < len(SMALL_WAITS):
            for k in SMALL_WAITS[i]:
                smalls[k].wait()
        for b in ready:
            normalise(b)
        if i == 1:
            query()
        for b in now:
            project(b)
        ready = now

    lane = lax.broadcasted_iota(jnp.int32, (part * q_len, proj), 1)
    ones = jnp.where(lane == 0, 1.0, 0.0).astype(jnp.bfloat16)
    for g in range(CORES * RINGS):
        r = g // CORES
        if g % CORES == 0:
            rest, last = all_q.at[pl.ds(0, part - 1)], all_q.at[0]
            pltpu.make_async_copy(rest, rest, q_sem.at[g]).wait()

            @pl.when(my_ring != r)
            def _():
                pltpu.make_async_copy(last, last, q_sem.at[g]).wait()

            forward(r).start()
        else:
            forward(r).wait()
        for b in ready:
            normalise(b)
        ready = []
        block = all_q[g * part:(g + 1) * part].reshape(part * q_len, proj)
        block = jnp.concatenate([block, ones], axis=1)
        best = None
        for b in range(0, tokens.shape[0], SCORE_ROWS):
            sim = lax.dot_general(tokens[b:b + SCORE_ROWS, :], block, (((1,), (1,)), ((), ())),
                                  preferred_element_type=jnp.float32)
            best_b = jnp.max(sim.reshape(SCORE_ROWS // 8, 8, part * q_len), axis=0)
            best = best_b if best is None else jnp.maximum(best, best_b)
        acc[g] = best

    top = jnp.max(acc[...], axis=1).reshape(group_size * q_len // 128, 128)
    per_row = 128 // q_len
    n_rows = group_size // per_row
    lane = lax.broadcasted_iota(jnp.int32, (n_rows, 128), 1)
    mine = jnp.zeros((1, 128), jnp.float32)
    for k in range(per_row):
        total = jnp.sum(jnp.where(lane // q_len == k, top, 0.0), axis=1, keepdims=True)
        mine += jnp.sum(jnp.where(lane == senders[k * n_rows:(k + 1) * n_rows, :], total, 0.0), axis=0, keepdims=True)
    column[...] = mine

    def s_copy(t):
        target = t + 1 - (me + group_size - 1 - t) // group_size
        return pltpu.make_async_remote_copy(
            src_ref=column, dst_ref=table.at[pl.ds(me, 1), :], send_sem=s_send_sem, recv_sem=s_sem,
            device_id={'data2': target // inner, 'data': target % inner}, device_id_type=MESH)

    for t in range(group_size - 1):
        s_copy(t).start()

    sent = all_q.at[pl.ds(0, n_chips - 1)]
    pltpu.make_async_copy(sent, sent, send_sem.at[0]).wait()
    others = table.at[pl.ds(0, group_size - 1), :]
    pltpu.make_async_copy(others, others, s_sem).wait()
    pltpu.make_async_copy(others, others, s_send_sem).wait()

    rows = lax.broadcasted_iota(jnp.int32, (group_size, 128), 0)
    out_ref[...] = jnp.where(rows == me, mine, table[...])


def finish(outer, inner, scores_ref, temp_ref, rows_ref, mean_ref):
    group_size = outer * inner
    me = lax.axis_index('data2') * inner + lax.axis_index('data')
    logits = scores_ref[...] / temp_ref[0]
    peak = jnp.max(logits, axis=0, keepdims=True)
    log_norm = peak + jnp.log(jnp.sum(jnp.exp(logits - peak), axis=0, keepdims=True))
    lane = lax.broadcasted_iota(jnp.int32, (group_size, 128), 1)
    own = lane == lax.broadcasted_iota(jnp.int32, (group_size, 128), 0)
    loss = log_norm - jnp.sum(jnp.where(own, logits, 0.0), axis=0, keepdims=True)
    lane = lane[:1]
    rows_ref[0] = jnp.sum(jnp.where(lane == me, loss, 0.0))
    mean_ref[0] = jnp.sum(jnp.where(lane < group_size, loss, 0.0)) / group_size


def solution(mesh):
    outer, inner = mesh.shape['data2'], mesh.shape['data']
    group_size = outer * inner

    def device_fn(q_hidden, d_hidden, w_proj, q_mask, d_mask, temperature):
        q_len, width = q_hidden.shape[1:]
        d_len, proj = d_hidden.shape[1], w_proj.shape[1]
        n_chunks = d_len // CHUNK
        smem = pl.BlockSpec(memory_space=pltpu.SMEM)
        vmem = pl.BlockSpec(memory_space=pltpu.VMEM)
        scores = pl.pallas_call(
            functools.partial(kernel, outer, inner),
            out_shape=pltpu.VMEM((group_size, 128), jnp.float32),
            in_specs=[pl.BlockSpec(memory_space=pl.ANY)] * 5,
            out_specs=vmem,
            scratch_shapes=[
                pltpu.VMEM((n_chunks, CHUNK, width), jnp.bfloat16),
                pltpu.VMEM((n_chunks, CHUNK, proj), jnp.float32),
                pltpu.VMEM((d_len, 2 * proj), jnp.bfloat16),
                pltpu.VMEM((group_size, q_len, proj), jnp.bfloat16),
                pltpu.VMEM((CORES * RINGS, 8, group_size // (CORES * RINGS) * q_len), jnp.float32),
                pltpu.VMEM((1, 128), jnp.float32),
                pltpu.VMEM((group_size, 128), jnp.float32),
                pltpu.VMEM((group_size, 128), jnp.int32),
                pltpu.VMEM(q_hidden.shape, q_hidden.dtype),
                pltpu.VMEM(w_proj.shape, w_proj.dtype),
                pltpu.VMEM(q_mask.shape, q_mask.dtype),
                pltpu.VMEM(d_mask.shape, d_mask.dtype),
                pltpu.SemaphoreType.DMA((4,)),
                pltpu.SemaphoreType.DMA((n_chunks,)),
                pltpu.SemaphoreType.DMA((1 + RINGS,)),
                pltpu.SemaphoreType.DMA((CORES * RINGS,)),
                pltpu.SemaphoreType.DMA,
                pltpu.SemaphoreType.DMA,
            ],
            compiler_params=pltpu.CompilerParams(collective_id=0, has_side_effects=True,
                                                 vmem_limit_bytes=60 * 1024 * 1024),
            name='colbert_loss',
        )(q_hidden, d_hidden, w_proj, q_mask, d_mask)
        return pl.pallas_call(
            functools.partial(finish, outer, inner),
            out_shape=(jax.ShapeDtypeStruct((1,), jnp.float32),) * 2,
            in_specs=[vmem, smem],
            out_specs=(smem, smem),
            compiler_params=pltpu.CompilerParams(vmem_limit_bytes=4 * 1024 * 1024),
            name='loss',
        )(scores, temperature.reshape(1))

    return jax.shard_map(
        device_fn,
        mesh=mesh,
        in_specs=(P(ROW_AXES), P(ROW_AXES), P(), P(ROW_AXES), P(ROW_AXES), P()),
        out_specs=(P(ROW_AXES), P('replica')),
        check_vma=False,
    )
```

time: 28.1 us -> 24.8 us (0.88)
  Pallas kernels: 26.7 us -> 23.4 us
    pallas_call x1, Pallas kernels: 25.2 us -> 22.7 us  [device_fn(): pl.pallas_call(functools.partial(kernel, outer, inner), out_shape=pltpu.V...]
    pallas_call x1, Pallas kernels: 1.44 us -> 0.69 us  [device_fn(): pl.pallas_call(functools.partial(finish, outer, inner), out_shape=(jax.Sh...]
where the time goes in v2:
time: 24.8 us; the launch traced here: 24.7 us
  Pallas kernels  23.4 us (94%)
  between operations  1.29 us (5%)
    pallas_call x1, Pallas kernels, device_fn(): pl.pallas_call(functools.partial(kernel, outer, inner), out_shape=pltpu.V...  22.7 us
    pallas_call x1, Pallas kernels, device_fn(): pl.pallas_call(functools.partial(finish, outer, inner), out_shape=(jax.Sh...  0.69 us

profile of v2, /device:TPU:97, one launch (start us, length us, event | category | flops | bytes accessed | tf_op | source)
XLA Modules:
  0.0 24.7 jit_solution(14807538458254110513)
XLA Ops:
  1.3 22.7 %colbert_loss.1.scores_ref = f32[32,128]{1,0:T(8,128)S(1)} custom-call(bf16[1,32,1024]{2,1,0:T(8,128)(2,1)} %q_hbm.1, bf16[1,8192,1024]{2,1,0:T(8,128)(2,1)} %d_ref.1, bf16[1024,128]{1,0:T(8,128)(2,1)} %w_hbm.1, s32[1,32]{1,0:T(1,128)} %qm_hbm.1, s32[1,8192]{1,0:T(1,128)} %dm_hbm.1), custom_call_target="tpu_custom_call" | custom-call | tf_op jit(solution)/shard_map/colbert_loss/pallas_call | solution.py:209
  24.0 0.7 %loss.1 = (f32[1]{0:T(128)}, f32[1]{0:T(128)}) custom-call(f32[32,128]{1,0:T(8,128)S(1)} %colbert_loss.1.scores_ref, f32[1]{0:T(128)} %bitcast.1.temp_ref), custom_call_target="tpu_custom_call" | custom-call | tf_op jit(solution)/shard_map/loss/pallas_call | solution.py:238

commit v3 on v2

--- a/solution.py
+++ b/solution.py
@@ -16,7 +16,7 @@
 LEVELS = 2
 RINGS = 1
 FIRST = 2
-STEPS = (1, 3, 4, 4, 4)
+STEPS = (1, 2, 4, 4, 5)
 SEND_STEP = 2
 SMALL_WAITS = ((0,), (1, 2, 3))
 SCORE_ROWS = 4096
@@ -83,7 +83,7 @@
     def q_copy(t):
         return pltpu.make_async_remote_copy(
             src_ref=all_q.at[my_slot], dst_ref=all_q.at[my_slot], send_sem=send_sem.at[0], recv_sem=q_sem.at[my_ring * CORES],
-            device_id=chip_id(other_chip(t)), device_id_type=MESH)
+            device_id=chip_id((my_place + n_chips // 2 + t + (t >= n_chips // 2)) % n_chips), device_id_type=MESH)
 
     def forward(r):
         return pltpu.make_async_remote_copy(
@@ -108,7 +108,7 @@
         now, chunks = chunks[:count], chunks[count:]
         if i == SEND_STEP:
             pl.semaphore_wait(barrier, n_chips)
-            for t in reversed(range(n_chips - 1)):
+            for t in range(n_chips - 1):
                 q_copy(t).start()
         for b in now:
             fetch(b).wait()
@@ -192,8 +192,8 @@
     own = lane == lax.broadcasted_iota(jnp.int32, (group_size, 128), 0)
     loss = log_norm - jnp.sum(jnp.where(own, logits, 0.0), axis=0, keepdims=True)
     lane = lane[:1]
-    rows_ref[0] = jnp.sum(jnp.where(lane == me, loss, 0.0))
-    mean_ref[0] = jnp.sum(jnp.where(lane < group_size, loss, 0.0)) / group_size
+    rows_ref[...] = jnp.sum(jnp.where(lane == me, loss, 0.0), axis=1)
+    mean_ref[...] = jnp.sum(jnp.where(lane < group_size, loss, 0.0), axis=1) / group_size
 
 
 def solution(mesh):
@@ -239,7 +239,7 @@
             functools.partial(finish, outer, inner),
             out_shape=(jax.ShapeDtypeStruct((1,), jnp.float32),) * 2,
             in_specs=[vmem, smem],
-            out_specs=(smem, smem),
+            out_specs=(vmem, vmem),
             compiler_params=pltpu.CompilerParams(vmem_limit_bytes=4 * 1024 * 1024),
             name='loss',
         )(scores, temperature.reshape(1))

time: 24.8 us -> 24.7 us (level)
  no operation moved by 1% of the time
where the time goes in v3:
time: 24.7 us; the launch traced here: 24.6 us
  Pallas kernels  23.4 us (95%)
  between operations  1.29 us (5%)
    pallas_call x1, Pallas kernels, device_fn(): pl.pallas_call(functools.partial(kernel, outer, inner), out_shape=pltpu.V...  22.7 us
    pallas_call x1, Pallas kernels, device_fn(): pl.pallas_call(functools.partial(finish, outer, inner), out_shape=(jax.Sh...  0.64 us

profile of v3, /device:TPU:97, one launch (start us, length us, event | category | flops | bytes accessed | tf_op | source)
XLA Modules:
  0.0 24.6 jit_solution(224462884435284673)
XLA Ops:
  1.3 22.7 %colbert_loss.1.scores_ref = f32[32,128]{1,0:T(8,128)S(1)} custom-call(bf16[1,32,1024]{2,1,0:T(8,128)(2,1)} %q_hbm.1, bf16[1,8192,1024]{2,1,0:T(8,128)(2,1)} %d_ref.1, bf16[1024,128]{1,0:T(8,128)(2,1)} %w_hbm.1, s32[1,32]{1,0:T(1,128)} %qm_hbm.1, s32[1,8192]{1,0:T(1,128)} %dm_hbm.1), custom_call_target="tpu_custom_call" | custom-call | tf_op jit(solution)/shard_map/colbert_loss/pallas_call | solution.py:209
  24.0 0.6 %loss.1 = (f32[1]{0:T(128)}, f32[1]{0:T(128)}) custom-call(f32[32,128]{1,0:T(8,128)S(1)} %colbert_loss.1.scores_ref, f32[1]{0:T(128)} %bitcast.1.temp_ref), custom_call_target="tpu_custom_call" | custom-call | tf_op jit(solution)/shard_map/loss/pallas_call | solution.py:238
